TPU v7x, 32 devices: a whole 2x2x4 slice. The times are simulated.
32 devices in a mesh: dp: 2 (over x), tp: 4 (over z), kvp: 4 (over y, core).
Axes of the slice: x: 2, y: 2, z: 4, core: 2. Of those that a mesh axis runs over, the one named last changes fastest.
Arguments:
- x_in: bfloat16 [32, 5120], P('dp'), parts along dimension 0
- ctx_len: int32 [32], P('dp'), parts along dimension 0
- g_attn: bfloat16 [5120], replicated
- g_mlp: bfloat16 [5120], replicated
- w_qkv: bfloat16 [5120, 6144], P(None, 'tp')
- w_o: bfloat16 [4096, 5120], P(('tp', 'kvp'))
- w_gate: bfloat16 [5120, 32768], P(None, ('tp', 'kvp'))
- w_up: bfloat16 [5120, 32768], P(None, ('tp', 'kvp'))
- w_down: bfloat16 [32768, 5120], P(('tp', 'kvp'))
- k_cache: bfloat16 [32, 1024, 8, 128], P('dp', 'kvp', 'tp'), parts along dimension 0
- v_cache: bfloat16 [32, 1024, 8, 128], P('dp', 'kvp', 'tp'), parts along dimension 0
Outputs:
- output 1: bfloat16 [32, 5120], P('dp'), parts along dimension 0
- output 2: bfloat16 [32, 1024, 8, 128], P('dp', 'kvp', 'tp'), parts along dimension 0
- output 3: bfloat16 [32, 1024, 8, 128], P('dp', 'kvp', 'tp'), parts along dimension 0
There are 2 independent parts. A program takes and returns all parts, laid end to end along the dimension named above; an argument that names none is the same for every part.
All inputs are finite; a program needn't handle non-finite values.
Results may differ from a plain program's by a relative error of at most 0.00832932.
Values sent between devices are 32-bit elements.
A program may use at most 1 GiB of HBM per device.

v0:
```python
import jax
import jax.numpy as jnp
from jax import lax
from jax.sharding import PartitionSpec as P

ROPE_THETA = 500000.0
EPS = 1e-5
NEG_FILL = -1e30


def rms_norm(values, gain_vec):
    x_f32 = values.astype(jnp.float32)
    inv_rms = lax.rsqrt(jnp.mean(x_f32 * x_f32, axis=-1, keepdims=True) + EPS)
    return (x_f32 * inv_rms * gain_vec.astype(jnp.float32)).astype(jnp.bfloat16)


def rope_tables(ctx_len, head_dim):
    inv_freq = ROPE_THETA ** (-2.0 * jnp.arange(head_dim // 2, dtype=jnp.float32) / head_dim)
    angles = ctx_len.astype(jnp.float32)[:, None] * inv_freq[None, :]
    return jnp.cos(angles), jnp.sin(angles)


def rotary(vectors, cos_t, sin_t):
    half_dim = vectors.shape[-1] // 2
    first_half = vectors[..., :half_dim]
    second_half = vectors[..., half_dim:]
    return jnp.concatenate([first_half * cos_t - second_half * sin_t, second_half * cos_t + first_half * sin_t], axis=-1)


def mlp_part(hidden, g_mlp, w_gate, w_up, w_down):
    normed = rms_norm(hidden, g_mlp)
    gate_pre = jnp.dot(normed, w_gate, preferred_element_type=jnp.float32)
    up_proj = jnp.dot(normed, w_up, preferred_element_type=jnp.float32)
    act_out = (jax.nn.silu(gate_pre) * up_proj).astype(jnp.bfloat16)
    return jnp.dot(act_out, w_down, preferred_element_type=jnp.float32)


def local_attention(x_in, ctx_len, g_attn, w_qkv, k_cache, v_cache, kvp_index):
    batch_rows, block_len, kv_local, head_dim = k_cache.shape
    group_size = w_qkv.shape[1] // (kv_local * head_dim) - 2
    normed = rms_norm(x_in, g_attn)
    qkv_all = jnp.dot(normed, w_qkv, preferred_element_type=jnp.float32).reshape(batch_rows, kv_local, group_size + 2, head_dim)
    cos_t, sin_t = rope_tables(ctx_len, head_dim)
    queries = rotary(qkv_all[:, :, :group_size], cos_t[:, None, None, :], sin_t[:, None, None, :]).astype(jnp.bfloat16)
    key_new = rotary(qkv_all[:, :, group_size], cos_t[:, None, :], sin_t[:, None, :]).astype(jnp.bfloat16)
    val_new = qkv_all[:, :, group_size + 1].astype(jnp.bfloat16)
    positions = kvp_index * block_len + jnp.arange(block_len)
    hit_mask = (positions[None, :] == ctx_len[:, None])[:, :, None, None]
    k_out = jnp.where(hit_mask, key_new[:, None], k_cache)
    v_out = jnp.where(hit_mask, val_new[:, None], v_cache)
    scores = jnp.einsum("bgrd,btgd->bgrt", queries, k_out, preferred_element_type=jnp.float32) * head_dim ** -0.5
    valid = (positions[None, :] <= ctx_len[:, None])[:, None, None, :]
    scores = jnp.where(valid, scores, NEG_FILL)
    local_max = jnp.max(scores, axis=-1)
    prob_w = jnp.exp(scores - local_max[..., None])
    local_sum = jnp.sum(prob_w, axis=-1)
    local_acc = jnp.einsum("bgrt,btgd->bgrd", prob_w.astype(jnp.bfloat16), v_out, preferred_element_type=jnp.float32)
    return local_max, local_sum, local_acc, k_out, v_out


def solution(mesh):
    x_spec = P("dp", None)
    cache_spec = P("dp", "kvp", "tp", None)
    model_axes = ("tp", "kvp")

    def layer_step(x_in, ctx_len, g_attn, g_mlp, w_qkv, w_o, w_gate, w_up, w_down, k_cache, v_cache):
        kvp_index = lax.axis_index("kvp")
        local_max, local_sum, local_acc, k_out, v_out = local_attention(x_in, ctx_len, g_attn, w_qkv, k_cache, v_cache, kvp_index)
        batch_rows = local_acc.shape[0]
        attn_width = local_acc.shape[1] * local_acc.shape[2] * local_acc.shape[3]
        rows_own = w_o.shape[0]
        global_max = lax.pmax(local_max, "kvp")
        rescale = jnp.exp(local_max - global_max)
        denom_sum = lax.psum(local_sum * rescale, "kvp")
        acc_part = (local_acc * rescale[..., None]).reshape(batch_rows, attn_width)
        acc_own = lax.psum_scatter(acc_part, "kvp", scatter_dimension=1, tiled=True)
        denom_rows = jnp.broadcast_to(denom_sum[..., None], local_acc.shape).reshape(batch_rows, attn_width)
        denom_own = lax.dynamic_slice_in_dim(denom_rows, kvp_index * rows_own, rows_own, axis=1)
        attn_own = (acc_own / denom_own).astype(jnp.bfloat16)
        attn_sum = lax.psum(jnp.dot(attn_own, w_o, preferred_element_type=jnp.float32), model_axes)
        hidden = (x_in.astype(jnp.float32) + attn_sum).astype(jnp.bfloat16)
        mlp_sum = lax.psum(mlp_part(hidden, g_mlp, w_gate, w_up, w_down), model_axes)
        x_out = (hidden.astype(jnp.float32) + mlp_sum).astype(jnp.bfloat16)
        return x_out, k_out, v_out

    in_specs = (x_spec, P("dp"), P(None), P(None), P(None, "tp"), P(model_axes, None), P(None, model_axes), P(None, model_axes), P(model_axes, None), cache_spec, cache_spec)
    return jax.shard_map(layer_step, mesh=mesh, in_specs=in_specs, out_specs=(x_spec, cache_spec, cache_spec), check_vma=False)
```

profile of v0, /device:TPU:0, one launch (start us, length us, event | category | flops | bytes accessed | tf_op | source)
XLA Modules:
  0.0 282.6 jit_solution(3024716770761145577)
XLA Ops:
  7.2 0.0 copy-start
  7.2 0.0 reduce-scatter.2.cloned.1.call-start
  7.2 1.2 fusion.15
  8.5 0.7 convert_element_type.53
  9.2 7.8 %fusion.23 = f32[16,1536]{1,0:T(8,128)S(1)} fusion(bf16[5120,1536]{1,0:T(8,128)(2,1)} %param.15, bf16[16,5120]{1,0:T(8,128)(2,1)} %param.11, f32[5120]{0:T(1024)S(1)} %convert_element_type.53, f32[16]{0:T(128)S(1)} %add_rsqrt_fusion.1), kind=kOutput, calls=%fused_computation.26 | convolution fusion | flops 251985920 | bytes 16011328 | tf_op jit(solution)/shard_map/dot_general | solution.py:42
  17.1 0.1 broadcast_compare_fusion.1
  17.2 0.1 multiply_cosine_fusion
  17.3 0.1 subtract_convert_fusion
  17.4 0.1 subtract_convert_fusion.1
  17.5 0.1 pad_maximum_fusion
  17.6 7.6 %broadcast_select_fusion.1 = (bf16[16,256,2,128]{3,2,1,0:T(2,128)(2,1)S(1)}, bf16[16,256,2,128]{3,2,1,0:T(2,128)(2,1)}) fusion(bf16[16,256,2,128]{3,2,1,0:T(2,128)(2,1)} %param.20, pred[16,256]{1,0:T(8,128)(4,1)S(1)} %get-tuple-element.14, bf16[16,2,128]{2,1,0:T(2,128)(2,1)S(1)} %pad_maximum_fusion, bf16[16,256,2,128]{3,2,1,0:T(2,128)(2,1)} %param.21, ...), kind=kLoop, calls=%fused_computation.1 | loop fusion | flops 2097152 | bytes 8409088 | tf_op jit(solution)/shard_map/jit(_where)/select_n | solution.py:49
  25.2 1.3 copy-done.2
  26.5 0.8 fusion.50
  27.3 12.7 %pmax.7 = f32[16,2,4]{2,1,0:T(2,128)S(1)} all-reduce(f32[16,2,4]{2,1,0:T(2,128)S(1)} %get-tuple-element.17), channel_id=1, replica_groups=mesh['dp'=2,'tp'=4,'kvp'=4] {'kvp'}, use_global_device_ids=true, to_apply=%region_2.3 | all-reduce | flops 128 | bytes 1024 | tf_op jit(solution)/shard_map/pmax | solution.py:72
  40.1 0.2 fusion.32
  40.3 2.0 fusion.11
  42.3 0.7 reshape.204
  43.0 0.0 reduce-scatter.2.cloned.1.call-update
  43.0 0.0 all-reduce.3.cloned.1.call-start
  43.1 10.1 %psum.21 = f32[16,2,4]{2,1,0:T(2,128)S(1)} all-reduce(f32[16,2,4]{2,1,0:T(2,128)S(1)} %bitcast.17), channel_id=1, replica_groups=mesh['dp'=2,'tp'=4,'kvp'=4] {'kvp'}, use_global_device_ids=true, to_apply=%region_5.6 | all-reduce | flops 128 | bytes 1024 | tf_op jit(solution)/shard_map/psum | solution.py:74
  53.2 0.1 broadcast_in_dim.43
  53.3 9.7 %reduce-scatter.2.cloned.1.call-done = f32[16,256]{1,0:T(8,128)} async-done(((f32[16,1024]{1,0:T(8,128)}), f32[16,256]{1,0:T(8,128)}) %reduce-scatter.2.cloned.1.call-update) | async-done | bytes 16400 | tf_op jit(solution)/shard_map/reduce_scatter | solution.py:76
  63.1 1.9 fusion.44
  64.9 0.0 all-reduce.3.cloned.1.call-update
  65.0 0.0 all-reduce.5.cloned.1.call-start
  65.0 92.6 %all-reduce.3.cloned.1.call-done = f32[16,5120]{1,0:T(8,128)} async-done(((f32[16,5120]{1,0:T(8,128)}), f32[16,5120]{1,0:T(8,128)}) %all-reduce.3.cloned.1.call-update) | async-done | bytes 327696 | tf_op jit(solution)/shard_map/psum | solution.py:80
  157.6 1.1 fusion.19
  158.8 8.5 %fusion.39 = f32[16,2048]{1,0:T(8,128)S(1)} fusion(bf16[5120,2048]{1,0:T(8,128)(2,1)} %param.17, bf16[16,5120]{1,0:T(8,128)(2,1)S(1)} %get-tuple-element.4, f32[5120]{0:T(1024)S(1)} %convert_element_type.61, f32[16]{0:T(128)S(1)} %add_rsqrt_fusion), kind=kOutput, calls=%fused_computation.41 | convolution fusion | flops 335872000 | bytes 21286976 | tf_op jit(solution)/shard_map/dot_general | solution.py:32
  167.3 16.7 %fusion.14 = f32[16,5120]{1,0:T(8,128)} fusion(bf16[2048,5120]{1,0:T(8,128)(2,1)} %param.19, bf16[5120,2048]{1,0:T(8,128)(2,1)} %param.18, f32[16,2048]{1,0:T(8,128)S(1)} %fusion.39, bf16[16,5120]{1,0:T(8,128)(2,1)S(1)} %get-tuple-element.4, f32[5120]{0:T(1024)S(1)} %convert_element_type.61, f32[16]{0:T(128)S(1)} %add_rsqrt_fusion), kind=kOutput, calls=%fused_computation.11 | convolution fusion | flops 671612928 | bytes 42586176 | tf_op jit(solution)/shard_map/dot_general | solution.py:35
  184.0 0.0 all-reduce.5.cloned.1.call-update
  184.0 90.4 %all-reduce.5.cloned.1.call-done = f32[16,5120]{1,0:T(8,128)} async-done(((f32[16,5120]{1,0:T(8,128)}), f32[16,5120]{1,0:T(8,128)}) %all-reduce.5.cloned.1.call-update) | async-done | bytes 327696 | tf_op jit(solution)/shard_map/psum | solution.py:82
  274.4 1.7 fusion.22
  (23 shorter events, 0.2 us)
Async XLA Ops:
  7.2 55.9 %copy-start = (bf16[256,5120]{1,0:T(8,128)(2,1)S(1)}, bf16[256,5120]{1,0:T(8,128)(2,1)}, u32[]{:S(2)}) copy-start(bf16[256,5120]{1,0:T(8,128)(2,1)} %param.16) | copy-start | bytes 7864324
  7.2 55.9 %reduce-scatter.2.cloned.1.call-start = ((), (), s32[]{:S(2)}) async-start(), calls=%async_computation.1 | async-start | bytes 81920 | tf_op jit(solution)/shard_map/reduce_scatter | solution.py:76
  9.2 7.9 %copy-start.5 = (s32[16]{0:T(128)S(1)}, s32[16]{0:T(128)}, u32[]{:S(2)}) copy-start(s32[16]{0:T(128)} %param.12) | copy-start | bytes 196
  25.2 1.3 copy-start.2
  42.3 22.7 %copy-start.4 = (bf16[5120]{0:T(1024)(128)(2,1)S(1)}, bf16[5120]{0:T(1024)(128)(2,1)}, u32[]{:S(2)}) copy-start(bf16[5120]{0:T(1024)(128)(2,1)} %param.14) | copy-start | bytes 30724
  42.3 115.3 %copy-start.3 = (bf16[16,5120]{1,0:T(8,128)(2,1)S(1)}, bf16[16,5120]{1,0:T(8,128)(2,1)}, u32[]{:S(2)}) copy-start(bf16[16,5120]{1,0:T(8,128)(2,1)} %param.11) | copy-start | bytes 491524
  43.0 114.6 %all-reduce.3.cloned.1.call-start = ((), (), s32[]{:S(2)}) async-start(), calls=%async_computation.2 | async-start | bytes 655360 | tf_op jit(solution)/shard_map/psum | solution.py:80
  65.0 209.4 %all-reduce.5.cloned.1.call-start = ((), (), s32[]{:S(2)}) async-start(), calls=%async_computation.3 | async-start | bytes 655360 | tf_op jit(solution)/shard_map/psum | solution.py:82
  167.3 108.8 %copy-start.1 = (bf16[256,5120]{1,0:T(8,128)(2,1)S(1)}, bf16[256,5120]{1,0:T(8,128)(2,1)}, u32[]{:S(2)}) copy-start(bf16[256,5120]{1,0:T(8,128)(2,1)} %param.16) | copy-start | bytes 7864324
Sparse Core Ops, SparseCore 0:
  43.1 19.8 reduce-scatter.1
  66.4 91.1 all-reduce.2
  184.1 90.2 all-reduce.4
where the time goes:
time: 283 us
  waiting for transfers between devices  193 us (68%)
  matrix products  37.6 us (13%)
  blocking collectives  22.9 us (8%)
  between operations  13.9 us (5%)
  other arithmetic  13.1 us (5%)
    psum x1, waiting for transfers between devices, layer_step(): lax.psum(jnp.dot(attn_own, w_o, preferred_element_type=jnp.float32), mode...  92.6 us
    psum x1, waiting for transfers between devices, layer_step(): lax.psum(mlp_part(hidden, g_mlp, w_gate, w_up, w_down), model_axes)  90.4 us
    dot_general x1, matrix products, mlp_part(): return jnp.dot(act_out, w_down, preferred_element_type=jnp.float32)  16.7 us
    pmax x1, blocking collectives, layer_step(): global_max = lax.pmax(local_max, 'kvp')  12.7 us
    psum x1, blocking collectives, layer_step(): denom_sum = lax.psum(local_sum * rescale, 'kvp')  10.1 us
    reduce_scatter x1, waiting for transfers between devices, layer_step(): acc_own = lax.psum_scatter(acc_part, 'kvp', scatter_dimension=1, tiled=True)  9.73 us
    dot_general x1, matrix products, mlp_part(): gate_pre = jnp.dot(normed, w_gate, preferred_element_type=jnp.float32)  8.47 us
    dot_general x1, matrix products, local_attention(): jnp.dot(normed, w_qkv, preferred_element_type=jnp.float32)  7.75 us
  transfers between devices with their start and end apart: 3, of which 3 were waited for; matrix products, arithmetic and copies ran while one was open for 0% of the time, Pallas kernels for 0%

commit v1 on v0

v1 whole, which is shorter than its diff:
```python
import functools

import jax
import jax.numpy as jnp
import numpy as np
from jax import lax
from jax.experimental import pallas as pl
from jax.experimental.pallas import tpu as pltpu
from jax.sharding import PartitionSpec as P

ROPE_THETA = 500000.0
EPS = 1e-5
NEG_FILL = -1e30
MESH = pl.DeviceIdType.MESH
BF = jnp.bfloat16
F32 = jnp.float32
LANES = 128
TILE = 256
VMEM_BYTES = 67_043_328


def _layer_kernel(dims, ctx_ref, x_hbm, ga_hbm, gm_hbm, freq_hbm, wqkv_hbm, wo_hbm, wg_hbm, wu_hbm, wd_hbm, k_hbm, v_hbm,
                  out_ref, new_ref,
                  w, xb, ga, gm, freq, xf, nrm, qkv, qs, kn, vn, sc, pr, accx, mlx, racc, rml, part, recv_a, recv_b, full, act,
                  sem_in, sem_qkv, sem_kv, sem_wo, sem_gu, sem_dn, s_x, r_x, s_a, r_a, s_b, r_b, s_c, r_c, s_d, r_d):
    batch, width, ff, kv_loc, group, head, block_len, n_tp, n_kvp = dims
    half = batch // 2
    chips = n_tp * n_kvp // 2
    piece = width // chips
    heads = kv_loc * group
    n_qkv = kv_loc * (group + 2) * head // TILE
    n_gu = ff // TILE
    n_dn = width // TILE
    rows_o = wo_hbm.shape[0]
    cols = kv_loc * block_len

    up0 = n_gu * width
    dn0 = 2 * n_gu * width
    kv0 = dn0 - 2 * width
    wo0 = dn0 + n_qkv * width

    tp = lax.axis_index("tp")
    kvp = lax.axis_index("kvp")
    core = kvp % 2
    y = kvp // 2
    me = tp * 2 + y
    pal = kvp + 1 - 2 * core

    def flip(bits):
        hi, lo = bits // 2, bits % 2
        z = tp
        if hi == 3:
            z = 3 - tp
        elif hi == 2:
            z = (tp + 2) % 4
        elif hi == 1:
            z = tp + 1 - 2 * (tp % 2)
        yy = 1 - y if lo else y
        return z, yy

    peers = [flip(b) for b in (7, 5, 3, 6, 4, 2, 1)]

    def at(z, k):
        return {"tp": z, "kvp": k}

    small = [pltpu.make_async_copy(s, d, sem_in.at[i]) for i, (s, d) in enumerate(((x_hbm, xb), (ga_hbm, ga), (freq_hbm, freq), (gm_hbm, gm)))]

    def qkv_copy(n):
        return pltpu.make_async_copy(wqkv_hbm.at[:, pl.ds(n * TILE, TILE)], w.at[pl.ds(dn0 + n * width, width), :], sem_qkv.at[n])

    def wo_copy(n):
        return pltpu.make_async_copy(wo_hbm.at[:, pl.ds(n * TILE, TILE)], w.at[pl.ds(wo0 + n * rows_o, rows_o), :], sem_wo)

    def gate_copy(j):
        return pltpu.make_async_copy(wg_hbm.at[:, pl.ds(j * TILE, TILE)], w.at[pl.ds(j * width, width), :], sem_gu.at[2 * j])

    def up_copy(j):
        return pltpu.make_async_copy(wu_hbm.at[:, pl.ds(j * TILE, TILE)], w.at[pl.ds(up0 + j * width, width), :], sem_gu.at[2 * j + 1])

    def dn_copy(n):
        return pltpu.make_async_copy(wd_hbm.at[:, pl.ds(n * TILE, TILE)], w.at[pl.ds(dn0 + n * ff, ff), :], sem_dn.at[n])

    k_copy = pltpu.make_async_copy(k_hbm, w.at[pl.ds(kv0, batch * cols), pl.ds(0, head)], sem_kv.at[0])
    v_copy = pltpu.make_async_copy(v_hbm, w.at[pl.ds(kv0, batch * cols), pl.ds(head, head)], sem_kv.at[1])

    for c in small:
        c.start()
    for n in range(n_qkv):
        qkv_copy(n).start()
    k_copy.start()
    v_copy.start()
    for n in range(n_dn):
        wo_copy(n).start()
    for j in range(n_gu - 2):
        gate_copy(j).start()
        up_copy(j).start()

    barrier = pltpu.get_barrier_semaphore()
    greet = [at(z, yy * 2 + core) for z, yy in peers] + [at(tp, pal), at(tp, (1 - y) * 2 + 1 - core)]
    for d in greet:
        pl.semaphore_signal(barrier, inc=1, device_id=d, device_id_type=MESH)

    for c in small:
        c.wait()
    xv = xb[...].astype(F32)
    inv = lax.rsqrt(jnp.mean(xv * xv, axis=-1, keepdims=True) + EPS)
    nrm[...] = (xv * inv * ga[...].reshape(1, width).astype(F32)).astype(BF)
    for r in range(2):
        xf[r] = xv[r * half:(r + 1) * half]

    rows_i = lax.broadcasted_iota(jnp.int32, (batch, head), 0)
    pos = jnp.zeros((batch, head), F32)
    for b in range(batch):
        pos = jnp.where(rows_i == b, ctx_ref[b].astype(F32), pos)
    angle = pos * freq[0:1, :]
    lane = lax.broadcasted_iota(jnp.int32, (batch, head), 1)
    cos_t = jnp.cos(angle)
    sin_t = jnp.sin(angle)
    sin_t = jnp.where(lane < head // 2, -sin_t, sin_t)

    def qkv_step(i, carry):
        for u in range(2):
            qkv_copy(2 * i + u).wait()
        for u in range(2):
            n = 2 * i + u
            qkv[n] = jnp.dot(nrm[...], w[pl.ds(dn0 + n * width, width), :], preferred_element_type=F32)
        return carry

    lax.fori_loop(0, n_qkv // 2, qkv_step, 0)

    def column(j):
        return qkv[j // 2, :, (j % 2) * head:(j % 2 + 1) * head]

    def rotary(v):
        return (v * cos_t + pltpu.roll(v, head // 2, 1) * sin_t).astype(BF).astype(F32)

    for g in range(kv_loc):
        base = g * (group + 2)
        for r in range(group):
            qs[pl.ds(g * group + r, batch, stride=heads), :] = rotary(column(base + r))
        key = rotary(column(base + group))
        val = column(base + group + 1).astype(BF).astype(F32)
        new_ref[g] = key
        new_ref[kv_loc + g] = val
        for r in range(group):
            kn[pl.ds(g * group + r, batch, stride=heads), :] = key
            vn[pl.ds(g * group + r, batch, stride=heads), :] = val

    k_copy.wait()
    v_copy.wait()
    scale = head ** -0.5
    for b in range(batch):
        q_b = qs[b * heads:(b + 1) * heads, :].astype(BF)
        k_b = w[pl.ds(kv0 + b * cols, cols), 0:head]
        sc[b] = lax.dot_general(q_b, k_b, (((1,), (1,)), ((), ())), preferred_element_type=F32)
    s_new = jnp.sum(qs[...] * kn[...], axis=-1, keepdims=True) * scale
    col_i = lax.broadcasted_iota(jnp.int32, (heads, cols), 1)
    row_i = lax.broadcasted_iota(jnp.int32, (heads, cols), 0)
    own = (col_i % kv_loc) == (row_i // group)
    t_i = col_i // kv_loc
    lane_h = lax.broadcasted_iota(jnp.int32, (heads, head), 1)
    p_new = []
    for b in range(batch):
        here = ctx_ref[b] - kvp * block_len
        fresh = s_new[b * heads:(b + 1) * heads]
        is_new = own & (t_i == here)
        s = jnp.where(is_new, fresh, sc[b] * scale)
        s = jnp.where(own & (t_i <= here), s, NEG_FILL)
        m = jnp.max(s, axis=-1, keepdims=True)
        p = jnp.exp(s - m)
        total = jnp.sum(p, axis=-1, keepdims=True)
        p_new.append(jnp.max(jnp.where(is_new, p, 0.0), axis=-1, keepdims=True).astype(BF).astype(F32))
        pr[b] = jnp.where(is_new, 0.0, p).astype(BF)
        mlx[pl.ds(b, heads, stride=batch), :] = jnp.where(lane_h < head // 2, m, total)
    for b in range(batch):
        v_b = w[pl.ds(kv0 + b * cols, cols), head:2 * head]
        o = jnp.dot(pr[b], v_b, preferred_element_type=F32)
        accx[pl.ds(b, heads, stride=batch), :] = o + p_new[b] * vn[b * heads:(b + 1) * heads, :]

    for j in range(n_gu - 2, n_gu):
        gate_copy(j).start()
        up_copy(j).start()
    late = [n for n in range(n_dn) if dn0 + (n + 1) * ff > wo0 and dn0 + n * ff < wo0 + n_dn * rows_o]
    for n in range(n_dn):
        if n not in late:
            dn_copy(n).start()

    pl.semaphore_wait(barrier, len(greet))
    rows = heads // n_kvp * batch
    sent = []
    for d in (3, 2, 1):
        to = (kvp + d) % n_kvp
        frm = (kvp + n_kvp - d) % n_kvp
        for i, (src, dst) in enumerate(((accx, racc), (mlx, rml))):
            c = pltpu.make_async_remote_copy(src.at[pl.ds(to * rows, rows), :], dst.at[kvp], s_x.at[2 * d - 2 + i], r_x.at[2 * d - 2 + i],
                                             device_id=at(tp, to), device_id_type=MESH)
            c.start()
            sent.append(c)
    mine = pl.ds(pl.multiple_of(kvp * rows, rows), rows)
    racc[kvp] = accx[mine, :]
    rml[kvp] = mlx[mine, :]
    for c in sent:
        c.wait()
    ml = [rml[i] for i in range(n_kvp)]
    top = functools.reduce(jnp.maximum, ml)
    wt = [jnp.exp(v[:, 0:1] - top[:, 0:1]) for v in ml]
    den = sum(a * v[:, head // 2:head // 2 + 1] for a, v in zip(wt, ml))
    num = sum(a * racc[i] for i, a in enumerate(wt))
    a_f = num / den
    a_own = jnp.concatenate([a_f[r * batch:(r + 1) * batch] for r in range(rows // batch)], axis=1).astype(BF)

    for n in range(n_dn):
        wo_copy(n).wait()
    for n in range(n_dn):
        r = jnp.dot(a_own, w[pl.ds(wo0 + n * rows_o, rows_o), :], preferred_element_type=F32)
        part[0, :, n * TILE:(n + 1) * TILE] = r[:half]
        part[1, :, n * TILE:(n + 1) * TILE] = r[half:]
    for n in late:
        dn_copy(n).start()

    def span(chip):
        return pl.ds(pl.multiple_of(chip * piece, LANES), piece)

    def all_reduce(step, finish):
        sends = []
        a = pltpu.make_async_remote_copy(part.at[1 - core], recv_a.at[step], s_a.at[step], r_a.at[step], device_id=at(tp, pal), device_id_type=MESH)
        a.start()
        a.wait_recv()
        part[core] = part[core] + recv_a[step]
        for i, (z, yy) in enumerate(peers):
            c = pltpu.make_async_remote_copy(part.at[core, :, span(z * 2 + yy)], recv_b.at[step, i], s_b.at[step, i], r_b.at[step, i],
                                             device_id=at(z, yy * 2 + core), device_id_type=MESH)
            c.start()
            sends.append(c)
        total = part[core, :, span(me)]
        for i in range(len(peers)):
            sends[i].wait_recv()
            total = total + recv_b[step, i]
        full[step, core, :, span(me)] = finish(total)
        outs, fwd = [], []
        own_view = full.at[step, core, :, span(me)]
        for i, (z, yy) in enumerate(peers):
            c = pltpu.make_async_remote_copy(own_view, own_view, s_c.at[step, i], r_c.at[step, i], device_id=at(z, yy * 2 + core), device_id_type=MESH)
            c.start()
            outs.append(c)

        def forward(i, chip):
            view = full.at[step, core, :, span(chip)]
            c = pltpu.make_async_remote_copy(view, view, s_d.at[step, i], r_d.at[step, i], device_id=at(tp, pal), device_id_type=MESH)
            c.start()
            fwd.append(c)

        forward(len(peers), me)
        for i in reversed(range(len(peers))):
            outs[i].wait_recv()
            forward(i, peers[i][0] * 2 + peers[i][1])
        for c in fwd:
            c.wait_recv()
        a.wait_send()
        for c in sends + outs + fwd:
            c.wait_send()

    def finish_attention(total):
        return (xf[core, :, span(me)] + total).astype(BF).astype(F32)

    all_reduce(0, finish_attention)

    gain = gm[...].reshape(1, width).astype(F32)
    hv = jnp.concatenate([full[0, 0], full[0, 1]], axis=0)
    inv2 = lax.rsqrt(jnp.mean(hv * hv, axis=-1, keepdims=True) + EPS)
    nrm[...] = (hv * inv2 * gain).astype(BF)

    def gu_step(j, carry):
        gate_copy(j).wait()
        up_copy(j).wait()
        g_v = jnp.dot(nrm[...], w[pl.ds(j * width, width), :], preferred_element_type=F32)
        u_v = jnp.dot(nrm[...], w[pl.ds(up0 + j * width, width), :], preferred_element_type=F32)
        act[j] = (jax.nn.silu(g_v) * u_v).astype(BF)
        return carry

    lax.fori_loop(0, n_gu, gu_step, 0)
    av = jnp.concatenate([act[j] for j in range(n_gu)], axis=1)

    def dn_step(i, carry):
        for u in range(2):
            dn_copy(2 * i + u).wait()
        for u in range(2):
            n = 2 * i + u
            r = jnp.dot(av, w[pl.ds(dn0 + n * ff, ff), :], preferred_element_type=F32)
            sl = pl.ds(pl.multiple_of(n * TILE, TILE), TILE)
            part[0, :, sl] = r[:half]
            part[1, :, sl] = r[half:]
        return carry

    lax.fori_loop(0, n_dn // 2, dn_step, 0)

    def finish_mlp(total):
        return (full[0, core, :, span(me)] + total).astype(BF).astype(F32)

    all_reduce(1, finish_mlp)
    out_ref[...] = jnp.concatenate([full[1, 0], full[1, 1]], axis=0).astype(BF)


def _cache_kernel(dims, ctx_ref, new_ref, k_hbm, v_hbm, ko_hbm, vo_hbm, kbuf, vbuf, sem_i, sem_o):
    batch, block_len, kv_loc, chunks = dims
    kvp = lax.axis_index("kvp")
    size = batch // chunks
    jobs = [(i, c) for c in range(chunks) for i in range(2)]

    def load(i, c):
        src, buf = ((k_hbm, kbuf), (v_hbm, vbuf))[i]
        sl = pl.ds(c * size, size)
        return pltpu.make_async_copy(src.at[sl], buf.at[sl], sem_i.at[i, c])

    def save(i, c):
        dst, buf = ((ko_hbm, kbuf), (vo_hbm, vbuf))[i]
        sl = pl.ds(c * size, size)
        return pltpu.make_async_copy(buf.at[sl], dst.at[sl], sem_o.at[i, c])

    for j in jobs:
        load(*j).start()
    for i, c in jobs:
        load(i, c).wait()
        buf = (kbuf, vbuf)[i]
        for b in range(c * size, (c + 1) * size):
            here = ctx_ref[b] - kvp * block_len

            @pl.when((here >= 0) & (here < block_len))
            def _():
                rows = [new_ref[i * kv_loc + g, b:b + 1, :] for g in range(kv_loc)]
                buf[b, jnp.clip(here, 0, block_len - 1)] = jnp.concatenate(rows, axis=0).astype(BF)

        save(i, c).start()
    for j in jobs:
        save(*j).wait()


def solution(mesh):
    n_tp, n_kvp = mesh.shape["tp"], mesh.shape["kvp"]
    x_spec = P("dp", None)
    cache_spec = P("dp", "kvp", "tp", None)
    model_axes = ("tp", "kvp")

    def layer_step(x_in, ctx_len, g_attn, g_mlp, w_qkv, w_o, w_gate, w_up, w_down, k_cache, v_cache):
        batch, block_len, kv_loc, head = k_cache.shape
        width = x_in.shape[1]
        ff = w_gate.shape[1]
        group = w_qkv.shape[1] // (kv_loc * head) - 2
        heads = kv_loc * group
        chips = n_tp * n_kvp // 2
        n_qkv, n_gu, n_dn = w_qkv.shape[1] // TILE, ff // TILE, width // TILE
        half = batch // 2
        rows = heads // n_kvp * batch
        freq = (ROPE_THETA ** (-2.0 * np.arange(head // 2) / head)).astype(np.float32)
        freq = jnp.asarray(np.tile(np.concatenate([freq, freq])[None], (8, 1)))
        flat = (batch * block_len * kv_loc, head)
        hbm = pl.BlockSpec(memory_space=pl.ANY)
        smem = pl.BlockSpec(memory_space=pltpu.SMEM)
        vmem = pl.BlockSpec(memory_space=pltpu.VMEM)
        dma = pltpu.SemaphoreType.DMA
        peers = chips - 1
        dims = (batch, width, ff, kv_loc, group, head, block_len, n_tp, n_kvp)
        x_out, new = pl.pallas_call(
            functools.partial(_layer_kernel, dims),
            out_shape=(jax.ShapeDtypeStruct((batch, width), BF), jax.ShapeDtypeStruct((2 * kv_loc, batch, head), F32)),
            in_specs=[smem] + [hbm] * 11,
            out_specs=(vmem, vmem),
            scratch_shapes=[
                pltpu.VMEM((3 * ff * width // TILE, TILE), BF),
                pltpu.VMEM((batch, width), BF),
                pltpu.VMEM((width,), BF),
                pltpu.VMEM((width,), BF),
                pltpu.VMEM((8, head), F32),
                pltpu.VMEM((2, half, width), F32),
                pltpu.VMEM((batch, width), BF),
                pltpu.VMEM((n_qkv, batch, TILE), F32),
                pltpu.VMEM((batch * heads, head), F32),
                pltpu.VMEM((batch * heads, head), F32),
                pltpu.VMEM((batch * heads, head), F32),
                pltpu.VMEM((batch, heads, kv_loc * block_len), F32),
                pltpu.VMEM((batch, heads, kv_loc * block_len), BF),
                pltpu.VMEM((batch * heads, head), F32),
                pltpu.VMEM((batch * heads, head), F32),
                pltpu.VMEM((n_kvp, rows, head), F32),
                pltpu.VMEM((n_kvp, rows, head), F32),
                pltpu.VMEM((2, half, width), F32),
                pltpu.VMEM((2, half, width), F32),
                pltpu.VMEM((2, peers, half, width // chips), F32),
                pltpu.VMEM((2, 2, half, width), F32),
                pltpu.VMEM((n_gu, batch, TILE), BF),
                dma((4,)), dma((n_qkv,)), dma((2,)), dma, dma((2 * n_gu,)), dma((n_dn,)),
                dma((6,)), dma((6,)), dma((2,)), dma((2,)),
                dma((2, peers)), dma((2, peers)), dma((2, peers)), dma((2, peers)), dma((2, peers + 1)), dma((2, peers + 1)),
            ],
            compiler_params=pltpu.CompilerParams(collective_id=0, has_side_effects=True, vmem_limit_bytes=VMEM_BYTES),
            name="layer",
        )(ctx_len, x_in, g_attn, g_mlp, freq, w_qkv, w_o, w_gate, w_up, w_down, k_cache.reshape(flat), v_cache.reshape(flat))
        chunks = 4
        k_out, v_out = pl.pallas_call(
            functools.partial(_cache_kernel, (batch, block_len, kv_loc, chunks)),
            out_shape=(jax.ShapeDtypeStruct(k_cache.shape, BF), jax.ShapeDtypeStruct(v_cache.shape, BF)),
            in_specs=[smem, vmem, hbm, hbm],
            out_specs=(hbm, hbm),
            scratch_shapes=[pltpu.VMEM(k_cache.shape, BF), pltpu.VMEM(v_cache.shape, BF), dma((2, chunks)), dma((2, chunks))],
            compiler_params=pltpu.CompilerParams(vmem_limit_bytes=VMEM_BYTES),
            name="cache",
        )(ctx_len, new, k_cache, v_cache)
        return x_out, k_out, v_out

    in_specs = (x_spec, P("dp"), P(None), P(None), P(None, "tp"), P(model_axes, None), P(None, model_axes), P(None, model_axes), P(model_axes, None), cache_spec, cache_spec)
    return jax.shard_map(layer_step, mesh=mesh, in_specs=in_specs, out_specs=(x_spec, cache_spec, cache_spec), check_vma=False)
```

time: 283 us -> 72.1 us (0.25)
  waiting for transfers between devices: 193 us -> 0 us
  Pallas kernels: 0 us -> 69.6 us
  matrix products: 37.6 us -> 0 us
  blocking collectives: 22.9 us -> 0 us
  between operations: 13.9 us -> 0.65 us
  other arithmetic: 13.1 us -> 0 us
    psum x2 -> x0, waiting for transfers between devices: 183 us -> none  [the longest x1 92.6 us: layer_step(): lax.psum(jnp.dot(attn_own, w_o, preferred_element_type=jnp.float32), mode...]
    pallas_call x0 -> x2, Pallas kernels: none -> 69.6 us  [the longest x1 65.3 us: layer_step(): pl.pallas_call(functools.partial(_layer_kernel, dims), out_shape=(jax.Sha...]
    dot_general x6 -> x0, matrix products: 37.6 us -> none  [the longest x1 16.7 us: mlp_part(): return jnp.dot(act_out, w_down, preferred_element_type=jnp.float32)]
    pmax x1 -> x0, blocking collectives: 12.7 us -> none  [layer_step(): global_max = lax.pmax(local_max, 'kvp')]
    psum x1 -> x0, blocking collectives: 10.1 us -> none  [layer_step(): denom_sum = lax.psum(local_sum * rescale, 'kvp')]
    reduce_scatter x1 -> x0, waiting for transfers between devices: 9.73 us -> none  [layer_step(): acc_own = lax.psum_scatter(acc_part, 'kvp', scatter_dimension=1, tiled=True)]
    select_n x1 -> x0, other arithmetic: 7.62 us -> none  [local_attention(): k_out = jnp.where(hit_mask, key_new[:, None], k_cache)]
  transfers between devices with their start and end apart: 3 -> 0, of which waited for: 3 -> 0; matrix products, arithmetic and copies ran while one was open for 0% -> 0% of each run, Pallas kernels for 0% -> 0%
where the time goes in v1:
time: 72.1 us; the launch traced here: 71.9 us
  Pallas kernels  69.6 us (97%)
  local copies, waits for them, and re-layouts  1.59 us (2%)
    pallas_call x1, Pallas kernels, layer_step(): pl.pallas_call(functools.partial(_layer_kernel, dims), out_shape=(jax.Sha...  65.3 us
    pallas_call x1, Pallas kernels, layer_step(): pl.pallas_call(functools.partial(_cache_kernel, (batch, block_len, kv_loc...  4.35 us
    unnamed x1, local copies, waits for them, and re-layouts  1.59 us

profile of v1, /device:TPU:0, one launch (start us, length us, event | category | flops | bytes accessed | tf_op | source)
XLA Modules:
  0.0 71.9 jit_solution(4568780235520457218)
XLA Ops:
  0.6 65.3 %layer.1 = (bf16[16,5120]{1,0:T(8,128)(2,1)}, f32[4,16,128]{2,1,0:T(8,128)}) custom-call(s32[16]{0:T(128)} %ctx_ref.3, bf16[16,5120]{1,0:T(8,128)(2,1)} %x_hbm.1, bf16[5120]{0:T(1024)(128)(2,1)} %ga_hbm.1, bf16[5120]{0:T(1024)(128)(2,1)} %gm_hbm.1, f32[8,128]{1,0:T(8,128)} %constant.2.clone.freq_hbm, bf16[5120,1536]{1,0:T(8,128)(2,1)} %wqkv_hbm.1, ...), custom_call_target="tpu_custom_call" | custom-call | tf_op jit(solution)/shard_map/layer/pallas_call | solution.py:363
  65.9 4.3 %cache.1 = (bf16[16,256,2,128]{3,2,1,0:T(2,128)(2,1)}, bf16[16,256,2,128]{3,2,1,0:T(2,128)(2,1)}) custom-call(s32[16]{0:T(128)} %ctx_ref.3, f32[4,16,128]{2,1,0:T(8,128)} %get-tuple-element.8.new_ref, bf16[16,256,2,128]{3,2,1,0:T(2,128)(2,1)} %k_hbm.1, bf16[16,256,2,128]{3,2,1,0:T(2,128)(2,1)} %v_hbm.1), custom_call_target="tpu_custom_call" | custom-call | tf_op jit(solution)/shard_map/cache/pallas_call | solution.py:399
  70.3 1.6 %copy.16 = bf16[16,5120]{1,0:T(8,128)(2,1)} copy(bf16[16,5120]{1,0:T(8,128)(2,1)} %get-tuple-element.14) | data formatting | bytes 327680

commit v2 on v1

v2 whole, which is shorter than its diff:
```python
import functools

import jax
import jax.numpy as jnp
import numpy as np
from jax import lax
from jax.experimental import pallas as pl
from jax.experimental.pallas import tpu as pltpu
from jax.sharding import PartitionSpec as P

ROPE_THETA = 500000.0
EPS = 1e-5
NEG_FILL = -1e30
MESH = pl.DeviceIdType.MESH
BF = jnp.bfloat16
F32 = jnp.float32
LANES = 128
TILE = 256
VMEM_BYTES = 67_043_328


class _Phase:
    def __init__(self):
        self.scope = None

    def __call__(self, name):
        if self.scope is not None:
            self.scope.__exit__(None, None, None)
        self.scope = None
        if name:
            self.scope = jax.named_scope(name)
            self.scope.__enter__()


def _layer_kernel(dims, ctx_hbm, x_hbm, ga_hbm, gm_hbm, freq_hbm, wqkv_hbm, wo_hbm, wg_hbm, wu_hbm, wd_hbm, k_hbm, v_hbm,
                  out_ref, new_ref,
                  ctx_ref, wg, wu, wd, xb, ga, gm, freq, xf, nrm, gmx, qkv, qs, kn, vn, sc, pr, accx, mlx, racc, rml, part, recv_a, recv_b, full,
                  ssb, acc_g, acc_u, act,
                  sem_in, sem_qkv, sem_kv, sem_wo, sem_gu, sem_dn, s_q, r_q, s_x, r_x, s_s, r_s, s_a, r_a, s_b, r_b, s_c, r_c, s_d, r_d):
    batch, width, ff, kv_loc, group, head, block_len, n_tp, n_kvp = dims
    half = batch // 2
    chips = n_tp * n_kvp // 2
    piece = width // chips
    block = 2 * piece
    tiles = block // TILE
    heads = kv_loc * group
    n_qkv = kv_loc * (group + 2) * head // TILE
    q_loc = n_qkv // 2
    n_gu = ff // TILE
    n_dn = width // TILE
    rows_o = wo_hbm.shape[0]
    cols = kv_loc * block_len
    kv0 = q_loc * width
    wo0 = kv0 + batch * cols
    wo_end = wo0 + n_dn * rows_o

    phase = _Phase()
    phase("loads")
    tp = lax.axis_index("tp")
    kvp = lax.axis_index("kvp")
    core = kvp % 2
    y = kvp // 2
    me = tp * 2 + y
    pal = kvp + 1 - 2 * core
    zs = [tp, tp + 1 - 2 * (tp % 2), (tp + 2) % 4, 3 - tp]
    ys = [y, 1 - y]
    cores = [core, 1 - core]

    def device(e, lo, cc=0):
        return {"tp": zs[e], "kvp": ys[lo] * 2 + cores[cc]}

    def remote(src, dst, send, recv, to):
        return pltpu.make_async_remote_copy(src, dst, send, recv, device_id=to, device_id_type=MESH)

    def aligned(start, size):
        return pl.ds(pl.multiple_of(start, LANES), size)

    small = [pltpu.make_async_copy(s, d, sem_in.at[i]) for i, (s, d) in enumerate(((x_hbm, xb), (ga_hbm, ga), (freq_hbm, freq), (ctx_hbm, ctx_ref), (gm_hbm, gm)))]

    def qkv_copy(n):
        return pltpu.make_async_copy(wqkv_hbm.at[:, aligned((core * q_loc + n) * TILE, TILE)], wd.at[pl.ds(n * width, width), :], sem_qkv.at[n])

    def wo_copy(n):
        return pltpu.make_async_copy(wo_hbm.at[:, pl.ds(n * TILE, TILE)], wd.at[pl.ds(wo0 + n * rows_o, rows_o), :], sem_wo)

    def gu_copy(e, i):
        src, dst = ((wg_hbm, wg), (wu_hbm, wu))[i]
        sl = pl.ds(pl.multiple_of(zs[e] * block, block), block)
        return pltpu.make_async_copy(src.at[sl, :], dst.at[sl, :], sem_gu.at[e, i])

    order = (3, 2, 1, 0)

    def dn_copy(slot):
        e, i = order[slot // tiles], slot % tiles
        return pltpu.make_async_copy(wd_hbm.at[:, aligned(zs[e] * block + i * TILE, TILE)], wd.at[pl.ds(slot * ff, ff), :], sem_dn.at[slot])

    k_copy = pltpu.make_async_copy(k_hbm, wd.at[pl.ds(kv0, batch * cols), pl.ds(0, head)], sem_kv.at[0])
    v_copy = pltpu.make_async_copy(v_hbm, wd.at[pl.ds(kv0, batch * cols), pl.ds(head, head)], sem_kv.at[1])

    for c in small:
        c.start()
    for n in range(q_loc):
        qkv_copy(n).start(priority=1)
    k_copy.start(priority=1)
    v_copy.start(priority=1)
    for n in range(n_dn):
        wo_copy(n).start(priority=1)
    for e in range(n_tp):
        for i in range(2):
            gu_copy(e, i).start(priority=1)

    barrier = pltpu.get_barrier_semaphore()
    greet = [(e, lo, cc) for e in range(n_tp) for lo in range(2) for cc in range(2)][1:]
    for g in greet:
        pl.semaphore_signal(barrier, inc=1, device_id=device(*g), device_id_type=MESH)

    phase("x_wait")
    for c in small:
        c.wait()
    phase("norm")
    xv = xb[...].astype(F32)
    inv = lax.rsqrt(jnp.mean(xv * xv, axis=-1, keepdims=True) + EPS)
    nrm[...] = (xv * inv * ga[...].reshape(1, width).astype(F32)).astype(BF)
    for r in range(2):
        xf[r] = xv[r * half:(r + 1) * half]
    gain = gm[...].reshape(1, width).astype(F32)
    for e in range(n_tp):
        gmx[e] = gain[:, e * block:(e + 1) * block]

    rows_i = lax.broadcasted_iota(jnp.int32, (batch, head), 0)
    lane = lax.broadcasted_iota(jnp.int32, (batch, head), 1)
    pos = jnp.zeros((batch, head), F32)
    for b in range(batch):
        pos = jnp.where(rows_i == b, ctx_ref[b].astype(F32), pos)
    angle = pos * freq[0:1, :]
    cos_t = jnp.cos(angle)
    sin_t = jnp.sin(angle)
    sin_t = jnp.where(lane < head // 2, -sin_t, sin_t)

    phase("barrier")
    pl.semaphore_wait(barrier, len(greet))
    phase("qkv")
    q_sends = []
    for n in range(q_loc):
        qkv_copy(n).wait()
        mid = width // 2
        lo_half = jnp.dot(nrm[:, :mid], wd[n * width:n * width + mid, :], preferred_element_type=F32)
        hi_half = jnp.dot(nrm[:, mid:], wd[n * width + mid:(n + 1) * width, :], preferred_element_type=F32)
        slot = core * q_loc + n
        qkv[slot] = lo_half + hi_half
        c = remote(qkv.at[slot], qkv.at[slot], s_q.at[n], r_q.at[n], device(0, 0, 1))
        c.start()
        q_sends.append(c)
    phase("qkv_swap")
    for c in q_sends:
        c.wait_recv()
    phase("rope")

    def column(j):
        return qkv[j // 2, :, (j % 2) * head:(j % 2 + 1) * head]

    def rotary(v):
        return (v * cos_t + pltpu.roll(v, head // 2, 1) * sin_t).astype(BF).astype(F32)

    for g in range(kv_loc):
        base = g * (group + 2)
        for r in range(group):
            qs[pl.ds(g * group + r, batch, stride=heads), :] = rotary(column(base + r))
        key = rotary(column(base + group))
        val = column(base + group + 1).astype(BF).astype(F32)
        new_ref[g] = key
        new_ref[kv_loc + g] = val
        for r in range(group):
            kn[pl.ds(g * group + r, batch, stride=heads), :] = key
            vn[pl.ds(g * group + r, batch, stride=heads), :] = val

    phase("kv_wait")
    k_copy.wait()
    v_copy.wait()
    phase("scores")
    scale = head ** -0.5
    for b in range(batch):
        q_b = qs[b * heads:(b + 1) * heads, :].astype(BF)
        k_b = wd[kv0 + b * cols:kv0 + (b + 1) * cols, 0:head]
        sc[b] = lax.dot_general(q_b, k_b, (((1,), (1,)), ((), ())), preferred_element_type=F32)
    phase("softmax")
    s_new = jnp.sum(qs[...] * kn[...], axis=-1, keepdims=True) * scale
    col_i = lax.broadcasted_iota(jnp.int32, (heads, cols), 1)
    row_i = lax.broadcasted_iota(jnp.int32, (heads, cols), 0)
    own = (col_i % kv_loc) == (row_i // group)
    t_i = col_i // kv_loc
    lane_h = lax.broadcasted_iota(jnp.int32, (heads, head), 1)
    p_new = []
    for b in range(batch):
        here = ctx_ref[b] - kvp * block_len
        fresh = s_new[b * heads:(b + 1) * heads]
        is_new = own & (t_i == here)
        s = jnp.where(is_new, fresh, sc[b] * scale)
        s = jnp.where(own & (t_i <= here), s, NEG_FILL)
        m = jnp.max(s, axis=-1, keepdims=True)
        p = jnp.exp(s - m)
        total = jnp.sum(p, axis=-1, keepdims=True)
        p_new.append(jnp.max(jnp.where(is_new, p, 0.0), axis=-1, keepdims=True).astype(BF).astype(F32))
        pr[b] = jnp.where(is_new, 0.0, p).astype(BF)
        mlx[pl.ds(b, heads, stride=batch), :] = jnp.where(lane_h < head // 2, m, total)
    phase("values")
    for b in range(batch):
        v_b = wd[kv0 + b * cols:kv0 + (b + 1) * cols, head:2 * head]
        o = jnp.dot(pr[b], v_b, preferred_element_type=F32)
        accx[pl.ds(b, heads, stride=batch), :] = o + p_new[b] * vn[b * heads:(b + 1) * heads, :]

    phase("exchange")
    rows = heads // n_kvp * batch
    sent = []
    for d, (lo, cc) in enumerate(((1, 1), (1, 0), (0, 1))):
        to = ys[lo] * 2 + cores[cc]
        for i, (src, dst) in enumerate(((accx, racc), (mlx, rml))):
            c = remote(src.at[pl.ds(pl.multiple_of(to * rows, rows), rows), :], dst.at[kvp], s_x.at[2 * d + i], r_x.at[2 * d + i], device(0, lo, cc))
            c.start()
            sent.append(c)
    early = [n for n in range(n_dn) if (n + 1) * ff <= wo0]
    for n in early:
        dn_copy(n).start(priority=1)
    mine = pl.ds(pl.multiple_of(kvp * rows, rows), rows)
    racc[kvp] = accx[mine, :]
    rml[kvp] = mlx[mine, :]
    for c in sent:
        c.wait()
    for c in q_sends:
        c.wait_send()
    phase("combine")
    ml = [rml[i] for i in range(n_kvp)]
    top = functools.reduce(jnp.maximum, ml)
    wt = [jnp.exp(v[:, 0:1] - top[:, 0:1]) for v in ml]
    den = sum(a * v[:, head // 2:head // 2 + 1] for a, v in zip(wt, ml))
    num = sum(a * racc[i] for i, a in enumerate(wt))
    a_f = num / den
    a_own = jnp.concatenate([a_f[r * batch:(r + 1) * batch] for r in range(rows // batch)], axis=1).astype(BF)

    def span(chip):
        return aligned(chip * piece, piece)

    def scatter_sum(step, tile):
        a, b = {}, {}

        def pass_on(e):
            a[e].wait_recv()
            sl = aligned(zs[e] * block, block)
            part[core, :, sl] = part[core, :, sl] + recv_a[step, e]
            for lo in (1, 0):
                i = 2 * e + lo - 1
                if i >= 0:
                    b[i] = remote(part.at[core, :, span(zs[e] * 2 + ys[lo])], recv_b.at[step, i], s_b.at[step, i], r_b.at[step, i], device(e, lo))
                    b[i].start()

        before = None
        for k, e in enumerate(order):
            tile(k, e)
            sl = aligned(zs[e] * block, block)
            a[e] = remote(part.at[1 - core, :, sl], recv_a.at[step, e], s_a.at[step, e], r_a.at[step, e], device(0, 0, 1))
            a[e].start()
            if before is not None:
                pass_on(before)
            before = e
        pass_on(before)
        phase("scatter")
        total = part[core, :, span(me)]
        for i in reversed(range(chips - 1)):
            b[i].wait_recv()
            total = total + recv_b[step, i]
        return total, list(a.values()) + list(b.values())

    def store_tile(e, i, r):
        sl = aligned(zs[e] * block + i * TILE, TILE)
        part[0, :, sl] = r[:half]
        part[1, :, sl] = r[half:]

    class Gather:
        def __init__(self, step, near_first):
            self.step = step
            self.out, self.fwd = {}, {}
            view = full.at[step, core, :, span(me)]
            todo = [(e, lo) for e in range(n_tp) for lo in (0, 1)][1:]
            for e, lo in todo if near_first else todo[::-1]:
                i = 2 * e + lo - 1
                self.out[e, lo] = remote(view, view, s_c.at[step, i], r_c.at[step, i], device(e, lo))
                self.out[e, lo].start()
            self.forward(0, 0)

        def forward(self, e, lo):
            view = full.at[self.step, core, :, span(zs[e] * 2 + ys[lo])]
            i = 2 * e + lo
            self.fwd[e, lo] = remote(view, view, s_d.at[self.step, i], r_d.at[self.step, i], device(0, 0, 1))
            self.fwd[e, lo].start()

        def arrive(self, e):
            for lo in (0, 1):
                if (e, lo) != (0, 0):
                    self.out[e, lo].wait_recv()
                    self.forward(e, lo)

        def settle(self, e):
            for lo in (0, 1):
                self.fwd[e, lo].wait_recv()

        def copies(self):
            return list(self.out.values()) + list(self.fwd.values())

    phase("wo")
    for n in range(n_dn):
        wo_copy(n).wait()

    def wo_tile(k, e):
        for i in range(tiles):
            at = pl.multiple_of(wo0 + (zs[e] * tiles + i) * rows_o, rows_o)
            store_tile(e, i, jnp.dot(a_own, wd[pl.ds(at, rows_o), :], preferred_element_type=F32))

    total, moving = scatter_sum(0, wo_tile)
    for n in range(n_dn):
        if n not in early:
            dn_copy(n).start(priority=1)
    h_own = (xf[core, :, span(me)] + total).astype(BF).astype(F32)
    full[0, core, :, span(me)] = h_own
    lane_p = lax.broadcasted_iota(jnp.int32, (half, LANES), 1)
    row_p = lax.broadcasted_iota(jnp.int32, (half, LANES), 0)
    squares = jnp.sum(h_own * h_own, axis=-1, keepdims=True)
    ss_id = me * 2 + core
    ssb[ss_id] = jnp.sum(jnp.where(lane_p == row_p, squares, 0.0), axis=0, keepdims=True)
    for i, g in enumerate(greet):
        c = remote(ssb.at[ss_id], ssb.at[ss_id], s_s.at[i], r_s.at[i], device(*g))
        c.start()
        moving.append(c)
    ss_copies = moving[-len(greet):]
    gather = Gather(0, True)
    moving += gather.copies()[:0]

    phase("gather_near")
    gather.arrive(0)
    gather.arrive(1)
    phase("squares")
    for c in ss_copies:
        c.wait_recv()
    sums = [sum(ssb[2 * q + c] for q in range(chips)) for c in range(2)]
    both = jnp.where(rows_i < half, sums[0], sums[1])
    mean = jnp.sum(jnp.where(lane == rows_i % half, both, 0.0), axis=-1, keepdims=True) / width
    inv2 = lax.rsqrt(mean + EPS)

    def gate_up(e):
        phase(f"gu_wait{e}")
        gather.settle(e)
        for i in range(2):
            gu_copy(e, i).wait()
        phase(f"gate_up{e}")
        sl = aligned(zs[e] * block, block)
        hv = jnp.concatenate([full[0, 0, :, sl], full[0, 1, :, sl]], axis=0)
        nv = (hv * inv2 * gmx[zs[e]]).astype(BF)
        wr = pl.ds(pl.multiple_of(zs[e] * block, block), block)
        for j in range(n_gu):
            g_v = jnp.dot(nv, wg[wr, j * TILE:(j + 1) * TILE], preferred_element_type=F32)
            u_v = jnp.dot(nv, wu[wr, j * TILE:(j + 1) * TILE], preferred_element_type=F32)
            if e > 0:
                g_v = acc_g[j] + g_v
                u_v = acc_u[j] + u_v
            if e < n_tp - 1:
                acc_g[j] = g_v
                acc_u[j] = u_v
            else:
                act[:, j * TILE:(j + 1) * TILE] = (jax.nn.silu(g_v) * u_v).astype(BF)

    gate_up(0)
    for e in range(1, n_tp):
        if e + 1 < n_tp:
            phase("gather")
            gather.arrive(e + 1)
        gate_up(e)
    for c in moving + gather.copies():
        c.wait_send()

    def dn_tile(k, e):
        phase(f"dn_wait{k}")
        for i in range(tiles):
            dn_copy(k * tiles + i).wait()
        phase(f"down{k}")
        for i in range(tiles):
            at = (k * tiles + i) * ff
            lo_half = jnp.dot(act[:, :ff // 2], wd[at:at + ff // 2, :], preferred_element_type=F32)
            hi_half = jnp.dot(act[:, ff // 2:], wd[at + ff // 2:at + ff, :], preferred_element_type=F32)
            store_tile(e, i, lo_half + hi_half)
        phase(f"pass{k}")

    total, moving = scatter_sum(1, dn_tile)
    full[1, core, :, span(me)] = (full[0, core, :, span(me)] + total).astype(BF).astype(F32)
    phase("gather2")
    last = Gather(1, False)
    for e in range(n_tp):
        last.arrive(e)
    phase("gather_core")
    for e in range(n_tp):
        last.settle(e)
    phase("output")
    out_ref[...] = jnp.concatenate([full[1, 0], full[1, 1]], axis=0).astype(BF)
    phase("drain")
    for c in moving + last.copies():
        c.wait_send()
    phase(None)


def _cache_kernel(dims, ctx_hbm, new_hbm, x_hbm, k_hbm, v_hbm, xo_hbm, ko_hbm, vo_hbm, ctx_ref, new_ref, xb, kbuf, vbuf, sem_s, sem_i, sem_o):
    batch, block_len, kv_loc, chunks = dims
    kvp = lax.axis_index("kvp")
    size = batch // chunks
    jobs = [(i, c) for c in range(chunks) for i in range(2)]

    def load(i, c):
        src, buf = ((k_hbm, kbuf), (v_hbm, vbuf))[i]
        sl = pl.ds(c * size, size)
        return pltpu.make_async_copy(src.at[sl], buf.at[sl], sem_i.at[i, c])

    def save(i, c):
        dst, buf = ((ko_hbm, kbuf), (vo_hbm, vbuf))[i]
        sl = pl.ds(c * size, size)
        return pltpu.make_async_copy(buf.at[sl], dst.at[sl], sem_o.at[i, c])

    small = [pltpu.make_async_copy(s, d, sem_s.at[i]) for i, (s, d) in enumerate(((ctx_hbm, ctx_ref), (new_hbm, new_ref), (x_hbm, xb)))]
    for c in small:
        c.start()
    for j in jobs:
        load(*j).start(priority=1)
    for c in small:
        c.wait()
    x_save = pltpu.make_async_copy(xb, xo_hbm, sem_s.at[3])
    x_save.start()
    for i, c in jobs:
        load(i, c).wait()
        buf = (kbuf, vbuf)[i]
        for b in range(c * size, (c + 1) * size):
            here = ctx_ref[b] - kvp * block_len

            @pl.when((here >= 0) & (here < block_len))
            def _():
                rows = [new_ref[i * kv_loc + g, b:b + 1, :] for g in range(kv_loc)]
                buf[b, jnp.clip(here, 0, block_len - 1)] = jnp.concatenate(rows, axis=0).astype(BF)

        save(i, c).start(priority=1)
    x_save.wait()
    for j in jobs:
        save(*j).wait()


def solution(mesh):
    n_tp, n_kvp = mesh.shape["tp"], mesh.shape["kvp"]
    x_spec = P("dp", None)
    cache_spec = P("dp", "kvp", "tp", None)
    model_axes = ("tp", "kvp")

    def layer_step(x_in, ctx_len, g_attn, g_mlp, w_qkv, w_o, w_gate, w_up, w_down, k_cache, v_cache):
        batch, block_len, kv_loc, head = k_cache.shape
        width = x_in.shape[1]
        ff = w_gate.shape[1]
        group = w_qkv.shape[1] // (kv_loc * head) - 2
        heads = kv_loc * group
        chips = n_tp * n_kvp // 2
        n_qkv, n_gu, n_dn = w_qkv.shape[1] // TILE, ff // TILE, width // TILE
        half = batch // 2
        rows = heads // n_kvp * batch
        freq = (ROPE_THETA ** (-2.0 * np.arange(head // 2) / head)).astype(np.float32)
        freq = jnp.asarray(np.tile(np.concatenate([freq, freq])[None], (8, 1)))
        flat = (batch * block_len * kv_loc, head)
        hbm = pl.BlockSpec(memory_space=pl.ANY)
        vmem = pl.BlockSpec(memory_space=pltpu.VMEM)
        dma = pltpu.SemaphoreType.DMA
        peers = chips - 1
        dims = (batch, width, ff, kv_loc, group, head, block_len, n_tp, n_kvp)
        x_out, new = pl.pallas_call(
            functools.partial(_layer_kernel, dims),
            out_shape=(jax.ShapeDtypeStruct((batch, width), BF), jax.ShapeDtypeStruct((2 * kv_loc, batch, head), F32)),
            in_specs=[hbm] * 12,
            out_specs=(vmem, vmem),
            scratch_shapes=[
                pltpu.SMEM((batch,), jnp.int32),
                pltpu.VMEM((width, ff), BF),
                pltpu.VMEM((width, ff), BF),
                pltpu.VMEM((ff * width // TILE, TILE), BF),
                pltpu.VMEM((batch, width), BF),
                pltpu.VMEM((width,), BF),
                pltpu.VMEM((width,), BF),
                pltpu.VMEM((8, head), F32),
                pltpu.VMEM((2, half, width), F32),
                pltpu.VMEM((batch, width), BF),
                pltpu.VMEM((n_tp, 1, width // n_tp), F32),
                pltpu.VMEM((n_qkv, batch, TILE), F32),
                pltpu.VMEM((batch * heads, head), F32),
                pltpu.VMEM((batch * heads, head), F32),
                pltpu.VMEM((batch * heads, head), F32),
                pltpu.VMEM((batch, heads, kv_loc * block_len), F32),
                pltpu.VMEM((batch, heads, kv_loc * block_len), BF),
                pltpu.VMEM((batch * heads, head), F32),
                pltpu.VMEM((batch * heads, head), F32),
                pltpu.VMEM((n_kvp, rows, head), F32),
                pltpu.VMEM((n_kvp, rows, head), F32),
                pltpu.VMEM((2, half, width), F32),
                pltpu.VMEM((2, n_tp, half, width // n_tp), F32),
                pltpu.VMEM((2, peers, half, width // chips), F32),
                pltpu.VMEM((2, 2, half, width), F32),
                pltpu.VMEM((n_tp * n_kvp, 1, LANES), F32),
                pltpu.VMEM((n_gu, batch, TILE), F32),
                pltpu.VMEM((n_gu, batch, TILE), F32),
                pltpu.VMEM((batch, ff), BF),
                dma((5,)), dma((n_qkv // 2,)), dma((2,)), dma, dma((n_tp, 2)), dma((n_dn,)),
                dma((n_qkv // 2,)), dma((n_qkv // 2,)), dma((6,)), dma((6,)), dma((n_tp * n_kvp - 1,)), dma((n_tp * n_kvp - 1,)),
                dma((2, n_tp)), dma((2, n_tp)), dma((2, peers)), dma((2, peers)), dma((2, peers)), dma((2, peers)),
                dma((2, peers + 1)), dma((2, peers + 1)),
            ],
            compiler_params=pltpu.CompilerParams(collective_id=0, has_side_effects=True, vmem_limit_bytes=VMEM_BYTES),
            name="layer",
        )(ctx_len, x_in, g_attn, g_mlp, freq, w_qkv, w_o, w_gate, w_up, w_down, k_cache.reshape(flat), v_cache.reshape(flat))
        chunks = 4
        x_out, k_out, v_out = pl.pallas_call(
            functools.partial(_cache_kernel, (batch, block_len, kv_loc, chunks)),
            out_shape=(jax.ShapeDtypeStruct((batch, width), BF), jax.ShapeDtypeStruct(k_cache.shape, BF), jax.ShapeDtypeStruct(v_cache.shape, BF)),
            in_specs=[hbm] * 5,
            out_specs=(hbm, hbm, hbm),
            scratch_shapes=[
                pltpu.SMEM((batch,), jnp.int32), pltpu.VMEM((2 * kv_loc, batch, head), F32), pltpu.VMEM((batch, width), BF),
                pltpu.VMEM(k_cache.shape, BF), pltpu.VMEM(v_cache.shape, BF), dma((4,)), dma((2, chunks)), dma((2, chunks)),
            ],
            compiler_params=pltpu.CompilerParams(vmem_limit_bytes=VMEM_BYTES),
            name="cache",
        )(ctx_len, new, x_out, k_cache, v_cache)
        return x_out, k_out, v_out

    in_specs = (x_spec, P("dp"), P(None), P(None), P(None, "tp"), P(model_axes, None), P(None, model_axes), P(None, model_axes), P(model_axes, None), cache_spec, cache_spec)
    return jax.shard_map(layer_step, mesh=mesh, in_specs=in_specs, out_specs=(x_spec, cache_spec, cache_spec), check_vma=False)
```

time: 72.1 us -> 57 us (0.79)
  Pallas kernels: 69.6 us -> 56.2 us
  local copies, waits for them, and re-layouts: 1.59 us -> 0 us
    pallas_call x1, Pallas kernels: 65.3 us -> 52.4 us  [layer_step(): pl.pallas_call(functools.partial(_layer_kernel, dims), out_shape=(jax.Sha...]
    unnamed x1 -> x0, local copies, waits for them, and re-layouts: 1.59 us -> none
where the time goes in v2:
time: 57 us; the launch traced here: 56.8 us
  Pallas kernels  56.2 us (99%)
  between operations  0.64 us (1%)
    pallas_call x1, Pallas kernels, layer_step(): pl.pallas_call(functools.partial(_layer_kernel, dims), out_shape=(jax.Sha...  52.4 us
    pallas_call x1, Pallas kernels, layer_step(): pl.pallas_call(functools.partial(_cache_kernel, (batch, block_len, kv_loc...  3.83 us

profile of v2, /device:TPU:0, one launch (start us, length us, event | category | flops | bytes accessed | tf_op | source)
XLA Modules:
  0.0 56.8 jit_solution(5351867402956672333)
XLA Ops:
  0.6 52.4 %layer.1 = (bf16[16,5120]{1,0:T(8,128)(2,1)}, f32[4,16,128]{2,1,0:T(8,128)}) custom-call(s32[16]{0:T(128)} %ctx_hbm.3, bf16[16,5120]{1,0:T(8,128)(2,1)} %x_hbm.1, bf16[5120]{0:T(1024)(128)(2,1)} %ga_hbm.1, bf16[5120]{0:T(1024)(128)(2,1)} %gm_hbm.1, f32[8,128]{1,0:T(8,128)} %constant.2.clone.freq_hbm, bf16[5120,1536]{1,0:T(8,128)(2,1)} %wqkv_hbm.1, ...), custom_call_target="tpu_custom_call" | custom-call | tf_op jit(solution)/shard_map/layer/pallas_call | solution.py:474
  53.0 3.8 %cache.1 = (bf16[16,5120]{1,0:T(8,128)(2,1)}, bf16[16,256,2,128]{3,2,1,0:T(2,128)(2,1)}, bf16[16,256,2,128]{3,2,1,0:T(2,128)(2,1)}) custom-call(s32[16]{0:T(128)} %ctx_hbm.3, f32[4,16,128]{2,1,0:T(8,128)} %get-tuple-element.5.new_hbm, bf16[16,5120]{1,0:T(8,128)(2,1)} %get-tuple-element.6.x_hbm, bf16[16,256,2,128]{3,2,1,0:T(2,128)(2,1)} %k_hbm.1, ...), custom_call_target="tpu_custom_call" | custom-call | tf_op jit(solution)/shard_map/cache/pallas_call | solution.py:518

commit v3 on v2

--- a/solution.py
+++ b/solution.py
@@ -34,9 +34,9 @@
 
 def _layer_kernel(dims, ctx_hbm, x_hbm, ga_hbm, gm_hbm, freq_hbm, wqkv_hbm, wo_hbm, wg_hbm, wu_hbm, wd_hbm, k_hbm, v_hbm,
                   out_ref, new_ref,
-                  ctx_ref, wg, wu, wd, xb, ga, gm, freq, xf, nrm, gmx, qkv, qs, kn, vn, sc, pr, accx, mlx, racc, rml, part, recv_a, recv_b, full,
+                  ctx_ref, wg, wu, wd, xb, ga, gm, freq, xf, nrm, gmx, qkv, qkv2, qs, kn, vn, sc, pr, accx, mlx, racc, rml, part, recv_a, recv_b, recv_c, full,
                   ssb, acc_g, acc_u, act,
-                  sem_in, sem_qkv, sem_kv, sem_wo, sem_gu, sem_dn, s_q, r_q, s_x, r_x, s_s, r_s, s_a, r_a, s_b, r_b, s_c, r_c, s_d, r_d):
+                  sem_in, sem_qkv, sem_kv, sem_wo, sem_gu, sem_dn, s_q, r_q, s_x, r_x, s_s, r_s, s_a, r_a, s_b, r_b, s_c, r_c, s_gz, r_gz, s_gy, r_gy, s_d, r_d):
     batch, width, ff, kv_loc, group, head, block_len, n_tp, n_kvp = dims
     half = batch // 2
     chips = n_tp * n_kvp // 2
@@ -105,7 +105,7 @@
     v_copy.start(priority=1)
     for n in range(n_dn):
         wo_copy(n).start(priority=1)
-    for e in range(n_tp):
+    def start_gu(e):
         for i in range(2):
             gu_copy(e, i).start(priority=1)
 
@@ -137,8 +137,7 @@
     sin_t = jnp.sin(angle)
     sin_t = jnp.where(lane < head // 2, -sin_t, sin_t)
 
-    phase("barrier")
-    pl.semaphore_wait(barrier, len(greet))
+    start_gu(0)
     phase("qkv")
     q_sends = []
     for n in range(q_loc):
@@ -146,8 +145,14 @@
         mid = width // 2
         lo_half = jnp.dot(nrm[:, :mid], wd[n * width:n * width + mid, :], preferred_element_type=F32)
         hi_half = jnp.dot(nrm[:, mid:], wd[n * width + mid:(n + 1) * width, :], preferred_element_type=F32)
+        qkv2[0, n] = lo_half
+        qkv2[1, n] = hi_half
+    start_gu(1)
+    phase("barrier")
+    pl.semaphore_wait(barrier, len(greet))
+    for n in range(q_loc):
         slot = core * q_loc + n
-        qkv[slot] = lo_half + hi_half
+        qkv[slot] = qkv2[0, n] + qkv2[1, n]
         c = remote(qkv.at[slot], qkv.at[slot], s_q.at[n], r_q.at[n], device(0, 0, 1))
         c.start()
         q_sends.append(c)
@@ -191,6 +196,7 @@
     t_i = col_i // kv_loc
     lane_h = lax.broadcasted_iota(jnp.int32, (heads, head), 1)
     p_new = []
+    stat = jnp.zeros((heads, head), F32)
     for b in range(batch):
         here = ctx_ref[b] - kvp * block_len
         fresh = s_new[b * heads:(b + 1) * heads]
@@ -202,7 +208,9 @@
         total = jnp.sum(p, axis=-1, keepdims=True)
         p_new.append(jnp.max(jnp.where(is_new, p, 0.0), axis=-1, keepdims=True).astype(BF).astype(F32))
         pr[b] = jnp.where(is_new, 0.0, p).astype(BF)
-        mlx[pl.ds(b, heads, stride=batch), :] = jnp.where(lane_h < head // 2, m, total)
+        stat = jnp.where(lane_h == b, m, jnp.where(lane_h == batch + b, total, stat))
+    for h in range(heads):
+        mlx[h] = stat[h:h + 1]
     phase("values")
     for b in range(batch):
         v_b = wd[kv0 + b * cols:kv0 + (b + 1) * cols, head:2 * head]
@@ -210,65 +218,83 @@
         accx[pl.ds(b, heads, stride=batch), :] = o + p_new[b] * vn[b * heads:(b + 1) * heads, :]
 
     phase("exchange")
-    rows = heads // n_kvp * batch
+    heads_o = heads // n_kvp
+    rows = heads_o * batch
     sent = []
     for d, (lo, cc) in enumerate(((1, 1), (1, 0), (0, 1))):
         to = ys[lo] * 2 + cores[cc]
-        for i, (src, dst) in enumerate(((accx, racc), (mlx, rml))):
-            c = remote(src.at[pl.ds(pl.multiple_of(to * rows, rows), rows), :], dst.at[kvp], s_x.at[2 * d + i], r_x.at[2 * d + i], device(0, lo, cc))
+        for i, (src, dst) in enumerate(((accx.at[pl.ds(pl.multiple_of(to * rows, rows), rows), :], racc), (mlx.at[pl.ds(to * heads_o, heads_o)], rml))):
+            c = remote(src, dst.at[kvp], s_x.at[2 * d + i], r_x.at[2 * d + i], device(0, lo, cc))
             c.start()
             sent.append(c)
-    early = [n for n in range(n_dn) if (n + 1) * ff <= wo0]
-    for n in early:
-        dn_copy(n).start(priority=1)
+    start_gu(2)
+    start_gu(3)
     mine = pl.ds(pl.multiple_of(kvp * rows, rows), rows)
     racc[kvp] = accx[mine, :]
-    rml[kvp] = mlx[mine, :]
+    rml[kvp] = mlx[pl.ds(kvp * heads_o, heads_o)]
     for c in sent:
         c.wait()
     for c in q_sends:
         c.wait_send()
     phase("combine")
-    ml = [rml[i] for i in range(n_kvp)]
-    top = functools.reduce(jnp.maximum, ml)
-    wt = [jnp.exp(v[:, 0:1] - top[:, 0:1]) for v in ml]
-    den = sum(a * v[:, head // 2:head // 2 + 1] for a, v in zip(wt, ml))
-    num = sum(a * racc[i] for i, a in enumerate(wt))
-    a_f = num / den
-    a_own = jnp.concatenate([a_f[r * batch:(r + 1) * batch] for r in range(rows // batch)], axis=1).astype(BF)
+    early = [n for n in range(n_dn) if (n + 1) * ff <= wo0]
+    for n in early:
+        dn_copy(n).start(priority=1)
+
+    def spread(row, shift):
+        return jnp.sum(jnp.where(lane == rows_i + shift, row, 0.0), axis=-1, keepdims=True)
+
+    parts = []
+    for r in range(heads_o):
+        m_s = [spread(rml[i, r], 0) for i in range(n_kvp)]
+        l_s = [spread(rml[i, r], batch) for i in range(n_kvp)]
+        top = functools.reduce(jnp.maximum, m_s)
+        wt = [jnp.exp(m - top) for m in m_s]
+        den = sum(a * l for a, l in zip(wt, l_s))
+        num = sum(a * racc[i, r * batch:(r + 1) * batch] for i, a in enumerate(wt))
+        parts.append(num / den)
+    a_own = jnp.concatenate(parts, axis=1).astype(BF)
 
     def span(chip):
         return aligned(chip * piece, piece)
 
     def scatter_sum(step, tile):
-        a, b = {}, {}
-
-        def pass_on(e):
+        a, b, c = {}, {}, {}
+
+        def to_y(e):
+            phase(f"core{e}")
             a[e].wait_recv()
             sl = aligned(zs[e] * block, block)
             part[core, :, sl] = part[core, :, sl] + recv_a[step, e]
-            for lo in (1, 0):
-                i = 2 * e + lo - 1
-                if i >= 0:
-                    b[i] = remote(part.at[core, :, span(zs[e] * 2 + ys[lo])], recv_b.at[step, i], s_b.at[step, i], r_b.at[step, i], device(e, lo))
-                    b[i].start()
-
-        before = None
-        for k, e in enumerate(order):
-            tile(k, e)
-            sl = aligned(zs[e] * block, block)
-            a[e] = remote(part.at[1 - core, :, sl], recv_a.at[step, e], s_a.at[step, e], r_a.at[step, e], device(0, 0, 1))
-            a[e].start()
-            if before is not None:
-                pass_on(before)
-            before = e
-        pass_on(before)
-        phase("scatter")
+            b[e] = remote(part.at[core, :, span(zs[e] * 2 + 1 - y)], recv_b.at[step, e], s_b.at[step, e], r_b.at[step, e], device(0, 1))
+            b[e].start()
+
+        def to_z(e):
+            phase(f"y{e}")
+            b[e].wait_recv()
+            sl = span(zs[e] * 2 + y)
+            part[core, :, sl] = part[core, :, sl] + recv_b[step, e]
+            if e > 0:
+                c[e] = remote(part.at[core, :, sl], recv_c.at[step, e - 1], s_c.at[step, e - 1], r_c.at[step, e - 1], device(e, 0))
+                c[e].start()
+
+        for k in range(n_tp + 2):
+            if k < n_tp:
+                e = order[k]
+                tile(k, e)
+                sl = aligned(zs[e] * block, block)
+                a[e] = remote(part.at[1 - core, :, sl], recv_a.at[step, e], s_a.at[step, e], r_a.at[step, e], device(0, 0, 1))
+                a[e].start()
+            if 0 <= k - 1 < n_tp:
+                to_y(order[k - 1])
+            if 0 <= k - 2 < n_tp:
+                to_z(order[k - 2])
+        phase("z")
         total = part[core, :, span(me)]
-        for i in reversed(range(chips - 1)):
-            b[i].wait_recv()
-            total = total + recv_b[step, i]
-        return total, list(a.values()) + list(b.values())
+        for e in order[:-1]:
+            c[e].wait_recv()
+            total = total + recv_c[step, e - 1]
+        return total, [*a.values(), *b.values(), *c.values()]
 
     def store_tile(e, i, r):
         sl = aligned(zs[e] * block + i * TILE, TILE)
@@ -276,35 +302,41 @@
         part[1, :, sl] = r[half:]
 
     class Gather:
-        def __init__(self, step, near_first):
+        def __init__(self, step):
             self.step = step
-            self.out, self.fwd = {}, {}
-            view = full.at[step, core, :, span(me)]
-            todo = [(e, lo) for e in range(n_tp) for lo in (0, 1)][1:]
-            for e, lo in todo if near_first else todo[::-1]:
-                i = 2 * e + lo - 1
-                self.out[e, lo] = remote(view, view, s_c.at[step, i], r_c.at[step, i], device(e, lo))
-                self.out[e, lo].start()
-            self.forward(0, 0)
-
-        def forward(self, e, lo):
-            view = full.at[self.step, core, :, span(zs[e] * 2 + ys[lo])]
-            i = 2 * e + lo
-            self.fwd[e, lo] = remote(view, view, s_d.at[self.step, i], r_d.at[self.step, i], device(0, 0, 1))
-            self.fwd[e, lo].start()
-
-        def arrive(self, e):
-            for lo in (0, 1):
-                if (e, lo) != (0, 0):
-                    self.out[e, lo].wait_recv()
-                    self.forward(e, lo)
+            self.zc, self.yc, self.fwd = {}, {}, {}
+            for e in (1, 2, 3):
+                self.zc[e] = self.copy(0, y, s_gz, r_gz, e - 1, device(e, 0))
+            self.along_y(0)
+            self.across(0, 0)
+
+        def copy(self, e, yy, send, recv, i, to):
+            view = full.at[self.step, core, :, span(zs[e] * 2 + yy)]
+            c = remote(view, view, send.at[self.step, i], recv.at[self.step, i], to)
+            c.start()
+            return c
+
+        def along_y(self, e):
+            self.yc[e] = self.copy(e, y, s_gy, r_gy, e, device(0, 1))
+
+        def across(self, e, lo):
+            self.fwd[e, lo] = self.copy(e, ys[lo], s_d, r_d, 2 * e + lo, device(0, 0, 1))
+
+        def from_z(self, e):
+            self.zc[e].wait_recv()
+            self.along_y(e)
+            self.across(e, 0)
+
+        def from_y(self, e):
+            self.yc[e].wait_recv()
+            self.across(e, 1)
 
         def settle(self, e):
             for lo in (0, 1):
                 self.fwd[e, lo].wait_recv()
 
         def copies(self):
-            return list(self.out.values()) + list(self.fwd.values())
+            return [*self.zc.values(), *self.yc.values(), *self.fwd.values()]
 
     phase("wo")
     for n in range(n_dn):
@@ -331,12 +363,11 @@
         c.start()
         moving.append(c)
     ss_copies = moving[-len(greet):]
-    gather = Gather(0, True)
-    moving += gather.copies()[:0]
+    gather = Gather(0)
 
     phase("gather_near")
-    gather.arrive(0)
-    gather.arrive(1)
+    gather.from_y(0)
+    gather.from_z(1)
     phase("squares")
     for c in ss_copies:
         c.wait_recv()
@@ -367,12 +398,18 @@
             else:
                 act[:, j * TILE:(j + 1) * TILE] = (jax.nn.silu(g_v) * u_v).astype(BF)
 
+    phase("gather_z")
+    gather.from_z(2)
+    gather.from_z(3)
     gate_up(0)
-    for e in range(1, n_tp):
-        if e + 1 < n_tp:
-            phase("gather")
-            gather.arrive(e + 1)
-        gate_up(e)
+    phase("gather_y1")
+    gather.from_y(1)
+    gate_up(1)
+    phase("gather_y2")
+    gather.from_y(2)
+    gather.from_y(3)
+    gate_up(2)
+    gate_up(3)
     for c in moving + gather.copies():
         c.wait_send()
 
@@ -383,17 +420,17 @@
         phase(f"down{k}")
         for i in range(tiles):
             at = (k * tiles + i) * ff
-            lo_half = jnp.dot(act[:, :ff // 2], wd[at:at + ff // 2, :], preferred_element_type=F32)
-            hi_half = jnp.dot(act[:, ff // 2:], wd[at + ff // 2:at + ff, :], preferred_element_type=F32)
-            store_tile(e, i, lo_half + hi_half)
-        phase(f"pass{k}")
+            store_tile(e, i, jnp.dot(act[...], wd[at:at + ff, :], preferred_element_type=F32))
 
     total, moving = scatter_sum(1, dn_tile)
     full[1, core, :, span(me)] = (full[0, core, :, span(me)] + total).astype(BF).astype(F32)
     phase("gather2")
-    last = Gather(1, False)
+    last = Gather(1)
+    for e in (1, 2, 3):
+        last.from_z(e)
+    phase("gather2_y")
     for e in range(n_tp):
-        last.arrive(e)
+        last.from_y(e)
     phase("gather_core")
     for e in range(n_tp):
         last.settle(e)
@@ -469,7 +506,6 @@
         hbm = pl.BlockSpec(memory_space=pl.ANY)
         vmem = pl.BlockSpec(memory_space=pltpu.VMEM)
         dma = pltpu.SemaphoreType.DMA
-        peers = chips - 1
         dims = (batch, width, ff, kv_loc, group, head, block_len, n_tp, n_kvp)
         x_out, new = pl.pallas_call(
             functools.partial(_layer_kernel, dims),
@@ -489,18 +525,20 @@
                 pltpu.VMEM((batch, width), BF),
                 pltpu.VMEM((n_tp, 1, width // n_tp), F32),
                 pltpu.VMEM((n_qkv, batch, TILE), F32),
+                pltpu.VMEM((2, n_qkv // 2, batch, TILE), F32),
                 pltpu.VMEM((batch * heads, head), F32),
                 pltpu.VMEM((batch * heads, head), F32),
                 pltpu.VMEM((batch * heads, head), F32),
                 pltpu.VMEM((batch, heads, kv_loc * block_len), F32),
                 pltpu.VMEM((batch, heads, kv_loc * block_len), BF),
                 pltpu.VMEM((batch * heads, head), F32),
-                pltpu.VMEM((batch * heads, head), F32),
+                pltpu.VMEM((heads, 1, head), F32),
                 pltpu.VMEM((n_kvp, rows, head), F32),
-                pltpu.VMEM((n_kvp, rows, head), F32),
+                pltpu.VMEM((n_kvp, heads // n_kvp, 1, head), F32),
                 pltpu.VMEM((2, half, width), F32),
                 pltpu.VMEM((2, n_tp, half, width // n_tp), F32),
-                pltpu.VMEM((2, peers, half, width // chips), F32),
+                pltpu.VMEM((2, n_tp, half, width // chips), F32),
+                pltpu.VMEM((2, n_tp - 1, half, width // chips), F32),
                 pltpu.VMEM((2, 2, half, width), F32),
                 pltpu.VMEM((n_tp * n_kvp, 1, LANES), F32),
                 pltpu.VMEM((n_gu, batch, TILE), F32),
@@ -508,8 +546,8 @@
                 pltpu.VMEM((batch, ff), BF),
                 dma((5,)), dma((n_qkv // 2,)), dma((2,)), dma, dma((n_tp, 2)), dma((n_dn,)),
                 dma((n_qkv // 2,)), dma((n_qkv // 2,)), dma((6,)), dma((6,)), dma((n_tp * n_kvp - 1,)), dma((n_tp * n_kvp - 1,)),
-                dma((2, n_tp)), dma((2, n_tp)), dma((2, peers)), dma((2, peers)), dma((2, peers)), dma((2, peers)),
-                dma((2, peers + 1)), dma((2, peers + 1)),
+                dma((2, n_tp)), dma((2, n_tp)), dma((2, n_tp)), dma((2, n_tp)), dma((2, n_tp - 1)), dma((2, n_tp - 1)),
+                dma((2, n_tp - 1)), dma((2, n_tp - 1)), dma((2, n_tp)), dma((2, n_tp)), dma((2, chips)), dma((2, chips)),
             ],
             compiler_params=pltpu.CompilerParams(collective_id=0, has_side_effects=True, vmem_limit_bytes=VMEM_BYTES),
             name="layer",

time: 57 us -> 61 us (1.070)
  Pallas kernels: 56.2 us -> 60.2 us
    pallas_call x1, Pallas kernels: 52.4 us -> 56.4 us  [layer_step(): pl.pallas_call(functools.partial(_layer_kernel, dims), out_shape=(jax.Sha...]
where the time goes in v3:
time: 61 us; the launch traced here: 60.9 us
  Pallas kernels  60.2 us (99%)
  between operations  0.64 us (1%)
    pallas_call x1, Pallas kernels, layer_step(): pl.pallas_call(functools.partial(_layer_kernel, dims), out_shape=(jax.Sha...  56.4 us
    pallas_call x1, Pallas kernels, layer_step(): pl.pallas_call(functools.partial(_cache_kernel, (batch, block_len, kv_loc...  3.83 us

profile of v3, /device:TPU:0, one launch (start us, length us, event | category | flops | bytes accessed | tf_op | source)
XLA Modules:
  0.0 60.9 jit_solution(3395350324762551473)
XLA Ops:
  0.6 56.4 %layer.1 = (bf16[16,5120]{1,0:T(8,128)(2,1)}, f32[4,16,128]{2,1,0:T(8,128)}) custom-call(s32[16]{0:T(128)} %ctx_hbm.3, bf16[16,5120]{1,0:T(8,128)(2,1)} %x_hbm.1, bf16[5120]{0:T(1024)(128)(2,1)} %ga_hbm.1, bf16[5120]{0:T(1024)(128)(2,1)} %gm_hbm.1, f32[8,128]{1,0:T(8,128)} %constant.2.clone.freq_hbm, bf16[5120,1536]{1,0:T(8,128)(2,1)} %wqkv_hbm.1, ...), custom_call_target="tpu_custom_call" | custom-call | tf_op jit(solution)/shard_map/layer/pallas_call | solution.py:510
  57.0 3.8 %cache.1 = (bf16[16,5120]{1,0:T(8,128)(2,1)}, bf16[16,256,2,128]{3,2,1,0:T(2,128)(2,1)}, bf16[16,256,2,128]{3,2,1,0:T(2,128)(2,1)}) custom-call(s32[16]{0:T(128)} %ctx_hbm.3, f32[4,16,128]{2,1,0:T(8,128)} %get-tuple-element.5.new_hbm, bf16[16,5120]{1,0:T(8,128)(2,1)} %get-tuple-element.6.x_hbm, bf16[16,256,2,128]{3,2,1,0:T(2,128)(2,1)} %k_hbm.1, ...), custom_call_target="tpu_custom_call" | custom-call | tf_op jit(solution)/shard_map/cache/pallas_call | solution.py:556
